TPU v7x, 256 devices: a whole 4x4x8 slice. The times are simulated.
256 devices in a mesh: rep: 1, dp: 256 (over x, y, z, core).
Axes of the slice: x: 4, y: 4, z: 8, core: 2. Of those that a mesh axis runs over, the one named last changes fastest.
Arguments:
- a: bfloat16 [256, 2, 2048, 1280], P(('rep', 'dp'))
- g: bfloat16 [256, 2, 2048, 3072], P(('rep', 'dp'))
Outputs:
- output: bfloat16 [2, 1280, 3072], P('rep')
All inputs are finite; a program needn't handle non-finite values.
Results may differ from a plain program's by a relative error of at most 0.012.
Values are sent between devices in bfloat16 or wider.
A program may use at most 768 MiB of HBM per device.

v0:
```python
import jax
import jax.numpy as jnp


def solution(mesh):
    groups = mesh.shape["rep"]

    def step(a, g):
        a, g = (t.reshape(groups, -1, *t.shape[1:]) for t in (a, g))
        sums = jnp.einsum("rsntd,rsntf->rndf", a, g, preferred_element_type=jnp.float32)
        return sums.astype(jnp.bfloat16).reshape(-1, *sums.shape[2:])

    return step
```

profile of v0, /device:TPU:1, one launch (start us, length us, event | category | flops | bytes accessed | tf_op | source)
XLA Modules:
  0.0 315.0 jit_solution(16816821205799273536)
XLA Ops:
  0.0 41.1 %fusion = f32[2,1280,3072]{2,1,0:T(8,128)} fusion(bf16[1,2,2048,3072]{3,2,1,0:T(8,128)(2,1)} %param.1, bf16[1,2,2048,1280]{3,2,1,0:T(8,128)(2,1)} %param), kind=kOutput, calls=%fused_computation | convolution fusion | flops 32212254720 | bytes 67108864 | tf_op jit(solution)/rsntd,rsntf->rndf/dot_general | solution.py:10
  41.1 273.9 %all-reduce.2 = bf16[2,1280,3072]{2,1,0:T(8,128)(2,1)} all-reduce(f32[2,1280,3072]{2,1,0:T(8,128)} %fusion), channel_id=1, replica_groups=mesh['axis_0'=256] {'axis_0'}, use_global_device_ids=true, to_apply=%add.clone | all-reduce | flops 7864320 | bytes 47185920 | tf_op jit(solution)/rsntd,rsntf->rndf/dot_general | solution.py:10
where the time goes:
time: 315 us
  blocking collectives  274 us (87%)
  matrix products  41.1 us (13%)
    dot_general x1, blocking collectives, step(): jnp.einsum('rsntd,rsntf->rndf', a, g, preferred_element_type=jnp.float32)  274 us
    dot_general x1, matrix products, step(): jnp.einsum('rsntd,rsntf->rndf', a, g, preferred_element_type=jnp.float32)  41.1 us

commit v1 on v0

v1 whole, which is shorter than its diff:
```python
import functools

import jax
import jax.numpy as jnp
from jax import lax
from jax.experimental import pallas as pl
from jax.experimental.pallas import tpu as pltpu
from jax.sharding import PartitionSpec as P

MESH = pl.DeviceIdType.MESH
BF16, F32 = jnp.bfloat16, jnp.float32
NX, NY, NZ = 4, 4, 8
SIZE = {"x": NX, "y": NY, "z": NZ}
CHUNKS = 5
UNIT = 256
WIDE = 3072
COLOUR = 1024
TILE = 512
TILES = WIDE // TILE
ORDER = ("xyz", "yxz", "zxy")
SLOTS = 272
HOPS = 17


def pos(h):
    return 6 + 2 * h


def add(a, n, k):
    return lax.rem(a + (k + n), n)


class Box:
    def __init__(self, row, rows, col, cols):
        self.row, self.rows, self.col, self.cols = row, rows, col, cols

    def half(self, h):
        if self.rows >= 32:
            r = self.rows // 2
            return Box(self.row + r * h, r, self.col, self.cols)
        c = self.cols // 2
        return Box(self.row, self.rows, self.col + c * h, c)


def at(ref, base, colour, box):
    row = base + box.row
    col = COLOUR * colour + box.col
    if not isinstance(row, int):
        row = pl.multiple_of(row, 16)
    if not isinstance(col, int):
        col = pl.multiple_of(col, 128)
    return ref.at[pl.ds(row, box.rows), pl.ds(col, box.cols)]


def block(colour, level, i, within):
    w = within
    if colour < 2:
        if level == 0:
            return Box(64 * i, 64, 0, 1024)
        if level == 1:
            return Box(w.row + 16 * i, 16, 0, 1024)
        return Box(w.row, 16, 128 * i, 128)
    if level == 0:
        return Box(32 * i, 32, 0, 1024)
    if level == 1:
        return Box(w.row + 16 * (i // 2), 16, 512 * lax.rem(i, 2), 512)
    return Box(w.row, 16, w.col + 128 * i, 128)


def landing(colour, level, way, s):
    if level == 0:
        full = 64 if colour < 2 else 32
        m = 2 if colour < 2 else 4
        rows = full // 2 if s == 0 else full
        row = way * (full // 2 + full * (m - 1)) + (0 if s == 0 else full // 2 + full * (s - 1))
        return Box(row, rows, 0, 1024)
    if level == 1:
        if colour < 2:
            if s == 0:
                return Box(192, 16, 512 * way, 512)
            return Box(208 + 16 * way, 16, 0, 1024)
        if s == 0:
            return Box(224, 16, 256 * way, 256)
        return Box(224 + 16 * way, 16, 512 * (1 - way), 512)
    row = 240 if colour < 2 else 256
    if way == 0:
        return Box(row, 16, 128 * s, 128)
    return Box(row, 16, 512 + 128 * s, 128)


def rows_loop(rows, body):
    if rows == 16:
        body(0)
    else:

        def step(i, _):
            body(pl.multiple_of(i * 16, 16))
            return 0

        lax.fori_loop(0, rows // 16, step, 0)


def kernel(a, g, G, av, gv, X, F, R, a_sem, g_sem, in_send, in_recv, hop_recv, ici_send, out_send, out_recv):
    me = lax.axis_index("dp")
    core = lax.rem(me, 2)
    place = {"x": me // (NY * NZ * 2), "y": lax.rem(me // (NZ * 2), NY), "z": lax.rem(me // 2, NZ)}

    def device(p, c):
        return ((p["x"] * NY + p["y"]) * NZ + p["z"]) * 2 + c

    def beside(axis, k):
        return device({**place, axis: add(place[axis], SIZE[axis], k)}, core)

    up = {d: beside(d, 1) for d in "xyz"}
    down = {d: beside(d, -1) for d in "xyz"}
    partner = me + 1 - 2 * core

    barrier = pltpu.get_barrier_semaphore()
    for peer in (*up.values(), *down.values(), partner):
        pl.semaphore_signal(barrier, inc=1, device_id={"dp": peer}, device_id_type=MESH)
    pl.semaphore_wait(barrier, 7)

    ahead = {d: jnp.where(core == 0, up[d], down[d]) for d in "xyz"}
    behind = {d: jnp.where(core == 0, down[d], up[d]) for d in "xyz"}
    sign = 1 - 2 * core

    def own_base(c):
        return 2 * UNIT * c + UNIT * core

    def send(src, dst, colour, recv, peer):
        pltpu.make_async_remote_copy(
            src, dst, ici_send.at[colour], recv, device_id={"dp": peer}, device_id_type=MESH
        ).start()

    def arrived(box, times, sem):
        view = X.at[pl.ds(0, box.rows * times), pl.ds(0, box.cols)]
        pltpu.make_async_copy(view, view, sem).wait()

    def load_a(c, slot):
        copies = []
        for h in range(2):
            unit = 2 * c + (core if h == 0 else 1 - core)
            n = unit // 5
            col = pl.multiple_of(UNIT * (unit - 5 * n), UNIT)
            copies.append(
                pltpu.make_async_copy(
                    a.at[0, n, :, pl.ds(col, UNIT)], av.at[slot, :, pl.ds(UNIT * h, UNIT)], a_sem.at[slot, h]
                )
            )
        return copies

    def load_g(c, t, h):
        unit = 2 * c + (core if h == 0 else 1 - core)
        slot = 2 * h + t % 2
        return pltpu.make_async_copy(g.at[0, unit // 5, :, pl.ds(TILE * t, TILE)], gv.at[slot], g_sem.at[slot])

    def fetch(c, t):
        load_g(c, t, 0).start()

        @pl.when(c == 2)
        def _():
            load_g(c, t, 1).start()

    def matmul(c, t):
        if t == 0:
            for copy in load_a(c, lax.rem(c, 2)):
                copy.wait()

            @pl.when(c + 1 < CHUNKS)
            def _():
                for copy in load_a(c + 1, lax.rem(c + 1, 2)):
                    copy.start()

        if t < TILES - 1:
            fetch(c, t + 1)
        else:

            @pl.when(c + 1 < CHUNKS)
            def _():
                fetch(c + 1, 0)

        load_g(c, t, 0).wait()

        @pl.when(c == 2)
        def _():
            load_g(c, t, 1).wait()

        slot = lax.rem(c, 2)
        other = jnp.where(c == 2, 2 + t % 2, t % 2)
        rows = pl.ds(pl.multiple_of(UNIT * c, UNIT), UNIT)
        cols = pl.ds(TILE * t, TILE)
        dims = (((0,), (0,)), ((), ()))
        theirs = lax.dot_general(av[slot, :, UNIT:], gv[other], dims, preferred_element_type=F32)
        X[rows, cols] = theirs.astype(BF16)
        there = pl.ds(pl.multiple_of(2 * UNIT * c + UNIT * (1 - core), UNIT), UNIT)
        pltpu.make_async_remote_copy(
            X.at[rows, cols],
            G.at[there, cols],
            in_send.at[c],
            in_recv.at[c],
            device_id={"dp": partner},
            device_id_type=MESH,
        ).start()
        F[rows, cols] = lax.dot_general(av[slot, :, :UNIT], gv[t % 2], dims, preferred_element_type=F32)

    def hop_reduce(c, k, level, s, path):
        axis = ORDER[k][level]
        n = SIZE[axis]
        m = n // 2
        p = place[axis]
        whole = level == 2
        x_base, g_base, r_base = UNIT * c, own_base(c), SLOTS * c
        ups, downs, sg = (ahead, behind, sign) if whole else (up, down, 1)
        within = path[level - 1] if level else None

        def own(box, r):
            b = Box(box.row + r, 16, box.col, box.cols)
            value = at(F, x_base, k, b)[...]
            if level == 0:
                value = value + at(G, g_base, k, b)[...].astype(F32)
            return value

        def got(box, r):
            return at(R, r_base, k, Box(box.row + r, 16, box.col, box.cols))[...].astype(F32)

        def put(box, extra):
            def body(r):
                value = own(box, r)
                if extra is not None:
                    value = value + got(extra, r)
                at(X, x_base, k, Box(box.row + r, 16, box.col, box.cols))[...] = value.astype(BF16)

            rows_loop(box.rows, body)

        def go(box, way, step):
            peer = (ups if way == 0 else downs)[axis]
            send(at(X, x_base, k, box), at(R, r_base, k, landing(k, level, way, step)), k, recv(level, step + 1), peer)

        def recv(lv, step):
            first = {0: 1, 1: 1 + SIZE[ORDER[k][0]] // 2, 2: 1 + (SIZE[ORDER[k][0]] + SIZE[ORDER[k][1]]) // 2}[lv]
            return hop_recv.at[c, k, first + step - 1]

        def blk(o):
            return block(k, level, add(p, n, sg * o), within)

        if s > 0:
            one = blk(0)
            if s == 1:
                arrived(one, 1, recv(level, s))
            else:
                arrived(one, 2, recv(level, s))
        if s == 0:
            far = blk(m)
            if whole:
                put(far, None)
                go(far, 0, 0)
            else:
                for way in range(2):
                    put(far.half(way), None)
                    go(far.half(way), way, 0)
        elif s < m:
            for way in range(2):
                box = blk((m - s) if way == 0 else -(m - s))
                if s == 1 and whole:
                    put(box, landing(k, level, 0, 0) if way == 0 else None)
                elif s == 1:
                    put(box.half(way), landing(k, level, way, 0))
                    put(box.half(1 - way), None)
                else:
                    put(box, landing(k, level, way, s - 1))
                go(box, way, s)
        else:
            box = blk(0)
            first, second = landing(k, level, 0, m - 1), landing(k, level, 1, m - 1)

            def body(r):
                value = own(box, r) + got(first, r) + got(second, r)
                b = Box(box.row + r, 16, box.col, box.cols)
                if whole:
                    at(G, g_base, k, b)[...] = value.astype(BF16)
                else:
                    at(F, x_base, k, b)[...] = value

            rows_loop(box.rows, body)

    def hop_gather(c, k, level, s, path):
        axis = ORDER[k][level]
        n = SIZE[axis]
        m = n // 2
        p = place[axis]
        whole = level == 2
        g_base = own_base(c)
        ups, downs, sg = (ahead, behind, sign) if whole else (up, down, 1)
        within = path[level - 1] if level else None
        sizes = [SIZE[d] // 2 for d in ORDER[k]]
        first = {2: 1 + sum(sizes), 1: 1 + sum(sizes) + sizes[2], 0: 1 + sum(sizes) + sizes[2] + sizes[1]}[level]

        def recv(step):
            return hop_recv.at[c, k, first + step - 1]

        def blk(o):
            return block(k, level, add(p, n, sg * o), within)

        def go(box, way, step):
            peer = (ups if way == 0 else downs)[axis]
            view = at(G, g_base, k, box)
            send(view, view, k, recv(step + 1), peer)

        def across(box):
            if level == 0:
                view = at(G, g_base, k, box)
                pltpu.make_async_remote_copy(
                    view, view, out_send, out_recv, device_id={"dp": partner}, device_id_type=MESH
                ).start()

        if s == 0:
            go(blk(0), 0, 0)
            go(blk(0), 1, 0)
            across(blk(0))
            return
        arrived(blk(0), 2 if s < m else 1, recv(s))
        if s == m:
            across(blk(m))
            return
        from_below, from_above = blk(-s), blk(s)
        if s < m - 1:
            go(from_below, 0, s)
            go(from_above, 1, s)
        elif whole:
            go(from_below, 0, s)
        else:
            go(from_below.half(0), 0, s)
            go(from_above.half(1), 1, s)
        across(from_below)
        across(from_above)

    def plan(k):
        sizes = [SIZE[d] // 2 for d in ORDER[k]]
        steps = [[] for _ in range(HOPS)]
        h = 0
        for level in range(3):
            for s in range(sizes[level] + 1):
                steps[h].append((hop_reduce, level, s))
                h += s < sizes[level]
        for level in (2, 1, 0):
            for s in range(sizes[level] + 1):
                steps[h].append((hop_gather, level, s))
                h += s < sizes[level]
        assert h == HOPS - 1
        return steps

    plans = [plan(k) for k in range(3)]

    def hop(h, c):
        if h == 0:
            view = X.at[pl.ds(0, UNIT), :]
            pltpu.make_async_copy(view, view, in_recv.at[c]).wait()
            pltpu.make_async_copy(view, view, in_send.at[c]).wait()
        for k in (2, 0, 1):
            path = []
            for level in range(3):
                path.append(block(k, level, place[ORDER[k][level]], path[-1] if path else None))
            for f, level, s in plans[k][h]:
                f(c, k, level, s, path)

    for copy in load_a(0, 0):
        copy.start()
    fetch(jnp.int32(0), 0)

    where = [(pos(h) // 6, pos(h) % 6) for h in range(HOPS)]
    last = max(j for j, _ in where)

    def iteration(i, _):
        for q in range(6):
            pl.when(i < CHUNKS)(functools.partial(matmul, i, q))
            for h in reversed(range(HOPS)):
                j, at_q = where[h]
                if at_q == q:
                    c = i - j
                    pl.when(jnp.logical_and(c >= 0, c < CHUNKS))(functools.partial(hop, h, c))
        return 0

    lax.fori_loop(0, CHUNKS + last, iteration, 0)

    half = X.at[pl.ds(0, CHUNKS * UNIT), :]
    pltpu.make_async_copy(half, half, out_recv).wait()
    pltpu.make_async_copy(half, half, out_send).wait()
    for k in range(3):
        view = G.at[pl.ds(0, 2032), pl.ds(0, 1280)]
        pltpu.make_async_copy(view, view, ici_send.at[k]).wait()


def unload(v, o, sem):
    copy = pltpu.make_async_copy(v, o, sem)
    copy.start()
    copy.wait()


def solution(mesh):
    def body(a, g):
        dma = pltpu.SemaphoreType.DMA
        held = pl.pallas_call(
            kernel,
            out_shape=pltpu.VMEM((2 * CHUNKS * UNIT, WIDE), BF16),
            in_specs=[pl.BlockSpec(memory_space=pltpu.HBM)] * 2,
            out_specs=pl.BlockSpec(memory_space=pltpu.VMEM),
            scratch_shapes=[
                pltpu.VMEM((2, 2048, 2 * UNIT), BF16),
                pltpu.VMEM((4, 2048, TILE), BF16),
                pltpu.VMEM((CHUNKS * UNIT, WIDE), BF16),
                pltpu.VMEM((CHUNKS * UNIT, WIDE), F32),
                pltpu.VMEM((CHUNKS * SLOTS, WIDE), BF16),
                dma((2, 2)),
                dma((4,)),
                dma((CHUNKS,)),
                dma((CHUNKS,)),
                dma((CHUNKS, 3, HOPS)),
                dma((3,)),
                dma,
                dma,
            ],
            compiler_params=pltpu.CompilerParams(
                collective_id=0, has_side_effects=True, vmem_limit_bytes=50_000_000
            ),
            name="sums",
        )(a, g)
        out = pl.pallas_call(
            unload,
            out_shape=jax.ShapeDtypeStruct(held.shape, held.dtype),
            in_specs=[pl.BlockSpec(memory_space=pltpu.VMEM)],
            out_specs=pl.BlockSpec(memory_space=pltpu.HBM),
            scratch_shapes=[dma],
            compiler_params=pltpu.CompilerParams(vmem_limit_bytes=1 << 20),
            name="unload",
        )(held)
        return out.reshape(2, CHUNKS * UNIT, WIDE)

    spec = P(("rep", "dp"))
    return jax.shard_map(body, mesh=mesh, in_specs=(spec, spec), out_specs=P("rep"), check_vma=False)
```

time: 315 us -> 152 us (0.48)
  blocking collectives: 274 us -> 0 us
  Pallas kernels: 0 us -> 151 us
  matrix products: 41.1 us -> 0 us
    dot_general x1 -> x0, blocking collectives: 274 us -> none  [step(): jnp.einsum('rsntd,rsntf->rndf', a, g, preferred_element_type=jnp.float32)]
    pallas_call x0 -> x2, Pallas kernels: none -> 151 us  [the longest x1 146 us: body(): pl.pallas_call(kernel, out_shape=pltpu.VMEM((2 * CHUNKS * UNIT, WIDE), BF...]
    dot_general x1 -> x0, matrix products: 41.1 us -> none  [step(): jnp.einsum('rsntd,rsntf->rndf', a, g, preferred_element_type=jnp.float32)]
where the time goes in v1:
time: 152 us; the launch traced here: 151 us
  Pallas kernels  151 us (99%)
    pallas_call x1, Pallas kernels, body(): pl.pallas_call(kernel, out_shape=pltpu.VMEM((2 * CHUNKS * UNIT, WIDE), BF...  146 us
    pallas_call x1, Pallas kernels, body(): pl.pallas_call(unload, out_shape=jax.ShapeDtypeStruct(held.shape, held.dt...  5.82 us

profile of v1, /device:TPU:1, one launch (start us, length us, event | category | flops | bytes accessed | tf_op | source)
XLA Modules:
  0.0 151.3 jit_solution(12321675196339816948)
XLA Ops:
  0.0 145.5 %sums.1.v = bf16[2560,3072]{1,0:T(8,128)(2,1)S(1)} custom-call(bf16[1,2,2048,1280]{3,2,1,0:T(8,128)(2,1)} %a.1, bf16[1,2,2048,3072]{3,2,1,0:T(8,128)(2,1)} %g.1), custom_call_target="tpu_custom_call" | custom-call | tf_op jit(solution)/shard_map/sums/pallas_call | solution.py:402
  145.5 5.8 %unload.1 = bf16[2560,3072]{1,0:T(8,128)(2,1)} custom-call(bf16[2560,3072]{1,0:T(8,128)(2,1)S(1)} %sums.1.v), custom_call_target="tpu_custom_call" | custom-call | tf_op jit(solution)/shard_map/unload/pallas_call | solution.py:427

commit v2 on v1

--- a/solution.py
+++ b/solution.py
@@ -19,11 +19,9 @@
 TILES = WIDE // TILE
 ORDER = ("xyz", "yxz", "zxy")
 SLOTS = 272
-HOPS = 17
-
-
-def pos(h):
-    return 6 + 2 * h
+LOADS = 4
+AHEAD = 2
+DIRECT = ((2,), (2,), (1, 2))
 
 
 def add(a, n, k):
@@ -65,6 +63,15 @@
     if level == 1:
         return Box(w.row + 16 * (i // 2), 16, 512 * lax.rem(i, 2), 512)
     return Box(w.row, 16, w.col + 128 * i, 128)
+
+
+def landing_direct(colour, level, o):
+    o -= 1
+    if level == 2:
+        return Box(240 if colour < 2 else 256, 16, 128 * o, 128)
+    if colour < 2:
+        return Box(192 + 16 * o, 16, 0, 1024)
+    return Box(224 + 16 * (o // 2), 16, 512 * (o % 2), 512)
 
 
 def landing(colour, level, way, s):
@@ -88,6 +95,70 @@
     return Box(row, 16, 512 + 128 * s, 128)
 
 
+FIRST = (-1, 3, 5, 9, 13, 15)
+
+
+def plan(k, direct):
+    hops = [[]]
+    for gather, levels in ((False, (0, 1, 2)), (True, (2, 1, 0))):
+        for level in levels:
+            steps = 1 if level in direct else SIZE[ORDER[k][level]] // 2
+            for s in range(steps + 1):
+                hops[-1].append((gather, level, s))
+                if s < steps:
+                    hops.append([])
+    return hops
+
+
+def messages(k, gather, level, s):
+    axis = ORDER[k][level]
+    n = SIZE[axis]
+    m = n // 2
+    full = UNIT * COLOUR * 2
+    for j in range(level + 1):
+        full //= SIZE[ORDER[k][j]]
+    if level in DIRECT[k]:
+        far = 0.75 * (m - 1)
+        return [(axis, 0, full * m * (m + 1) // 2, far), (axis, 1, full * m * (m - 1) // 2, far)] if s == 0 else []
+    if s == m:
+        return []
+    if s == (m - 1 if gather else 0):
+        full //= 2
+    return [(axis, 0, full, 0), (axis, 1, full, 0)]
+
+
+def sequence():
+    latency, rate, tile_time, hop_time = 2.3, 46.6e3, 1.5, 0.035
+    plans = [plan(k, DIRECT[k]) for k in range(3)]
+    free, arrival, order = {}, {}, []
+    now, tile = 3.5, 0
+    while True:
+        waiting = [x for x in arrival if arrival[x] is not None and x not in order]
+        ready = [x for x in waiting if arrival[x] <= now]
+        if ready:
+            c, k, h = x = min(ready, key=lambda x: (arrival[x] + 2 * x[0], x))
+            order.append(x)
+            spent = hop_time + 0.1 * (h == 0)
+            for gather, level, s in plans[k][h]:
+                spent += 0.08 * (level == 0 and not gather)
+                for axis, way, size, extra in messages(k, gather, level, s):
+                    end = max(now + spent, free.get((axis, way), 0)) + size / rate
+                    free[axis, way] = end
+                    to = c, k, h + 1
+                    arrival[to] = max(arrival.get(to, 0), end + latency + extra)
+            now += spent
+        elif tile < CHUNKS * TILES:
+            order.append(None)
+            now += tile_time
+            tile += 1
+            if tile % (TILES // 3) == 0:
+                arrival[(tile - 1) // TILES, (tile - 1) % TILES // (TILES // 3), 0] = now + 1.8
+        elif waiting:
+            now = min(arrival[x] for x in waiting)
+        else:
+            return order
+
+
 def rows_loop(rows, body):
     if rows == 16:
         body(0)
@@ -114,27 +185,6 @@
     up = {d: beside(d, 1) for d in "xyz"}
     down = {d: beside(d, -1) for d in "xyz"}
     partner = me + 1 - 2 * core
-
-    barrier = pltpu.get_barrier_semaphore()
-    for peer in (*up.values(), *down.values(), partner):
-        pl.semaphore_signal(barrier, inc=1, device_id={"dp": peer}, device_id_type=MESH)
-    pl.semaphore_wait(barrier, 7)
-
-    ahead = {d: jnp.where(core == 0, up[d], down[d]) for d in "xyz"}
-    behind = {d: jnp.where(core == 0, down[d], up[d]) for d in "xyz"}
-    sign = 1 - 2 * core
-
-    def own_base(c):
-        return 2 * UNIT * c + UNIT * core
-
-    def send(src, dst, colour, recv, peer):
-        pltpu.make_async_remote_copy(
-            src, dst, ici_send.at[colour], recv, device_id={"dp": peer}, device_id_type=MESH
-        ).start()
-
-    def arrived(box, times, sem):
-        view = X.at[pl.ds(0, box.rows * times), pl.ds(0, box.cols)]
-        pltpu.make_async_copy(view, view, sem).wait()
 
     def load_a(c, slot):
         copies = []
@@ -149,59 +199,93 @@
             )
         return copies
 
-    def load_g(c, t, h):
+    def place_g(i, h):
+        return lax.rem(i, AHEAD) + AHEAD * h
+
+    def load_g(i, h):
+        c = i // TILES
         unit = 2 * c + (core if h == 0 else 1 - core)
-        slot = 2 * h + t % 2
-        return pltpu.make_async_copy(g.at[0, unit // 5, :, pl.ds(TILE * t, TILE)], gv.at[slot], g_sem.at[slot])
-
-    def fetch(c, t):
-        load_g(c, t, 0).start()
+        slot = place_g(i, h)
+        cols = pl.ds(pl.multiple_of(TILE * (i - TILES * c), TILE), TILE)
+        return pltpu.make_async_copy(g.at[0, unit // 5, :, cols], gv.at[slot], g_sem.at[slot])
+
+    def fetch(i):
+        load_g(i, 0).start()
+
+        @pl.when(i // TILES == 2)
+        def _():
+            load_g(i, 1).start()
+
+    for copy in load_a(0, 0):
+        copy.start()
+    for i in range(AHEAD - 1):
+        fetch(jnp.int32(i))
+
+    peers = [beside(d, o) for d in "xyz" for o in range(1, SIZE[d])] + [partner]
+    barrier = pltpu.get_barrier_semaphore()
+    for peer in peers:
+        pl.semaphore_signal(barrier, inc=1, device_id={"dp": peer}, device_id_type=MESH)
+    ahead = {d: jnp.where(core == 0, up[d], down[d]) for d in "xyz"}
+    behind = {d: jnp.where(core == 0, down[d], up[d]) for d in "xyz"}
+    sign = 1 - 2 * core
+
+    def own_base(c):
+        return 2 * UNIT * c + UNIT * core
+
+    def send(src, dst, colour, recv, peer):
+        pltpu.make_async_remote_copy(
+            src, dst, ici_send.at[colour], recv, device_id={"dp": peer}, device_id_type=MESH
+        ).start()
+
+    def arrived(box, times, sem):
+        view = X.at[pl.ds(0, box.rows * times), pl.ds(0, box.cols)]
+        pltpu.make_async_copy(view, view, sem).wait()
+
+    def matmul(i, first=False):
+        c = i // TILES
+        q = i - TILES * c
+        slot = lax.rem(c, 2)
+
+        @pl.when(q == 0)
+        def _():
+            for copy in load_a(c, slot):
+                copy.wait()
+
+            @pl.when(c + 1 < CHUNKS)
+            def _():
+                for copy in load_a(c + 1, 1 - slot):
+                    copy.start()
+
+        @pl.when(i + AHEAD - 1 < CHUNKS * TILES)
+        def _():
+            fetch(i + AHEAD - 1)
+
+        load_g(i, 0).wait()
 
         @pl.when(c == 2)
         def _():
-            load_g(c, t, 1).start()
-
-    def matmul(c, t):
-        if t == 0:
-            for copy in load_a(c, lax.rem(c, 2)):
-                copy.wait()
-
-            @pl.when(c + 1 < CHUNKS)
-            def _():
-                for copy in load_a(c + 1, lax.rem(c + 1, 2)):
-                    copy.start()
-
-        if t < TILES - 1:
-            fetch(c, t + 1)
-        else:
-
-            @pl.when(c + 1 < CHUNKS)
-            def _():
-                fetch(c + 1, 0)
-
-        load_g(c, t, 0).wait()
-
-        @pl.when(c == 2)
-        def _():
-            load_g(c, t, 1).wait()
-
-        slot = lax.rem(c, 2)
-        other = jnp.where(c == 2, 2 + t % 2, t % 2)
+            load_g(i, 1).wait()
+
+        mine = place_g(i, 0)
+        other = mine + jnp.where(c == 2, AHEAD, 0)
         rows = pl.ds(pl.multiple_of(UNIT * c, UNIT), UNIT)
-        cols = pl.ds(TILE * t, TILE)
+        cols = pl.ds(pl.multiple_of(TILE * q, TILE), TILE)
         dims = (((0,), (0,)), ((), ()))
         theirs = lax.dot_general(av[slot, :, UNIT:], gv[other], dims, preferred_element_type=F32)
         X[rows, cols] = theirs.astype(BF16)
+        if first:
+            pl.semaphore_wait(barrier, len(peers))
         there = pl.ds(pl.multiple_of(2 * UNIT * c + UNIT * (1 - core), UNIT), UNIT)
+        k = q // (TILES // 3)
         pltpu.make_async_remote_copy(
             X.at[rows, cols],
             G.at[there, cols],
-            in_send.at[c],
-            in_recv.at[c],
+            in_send.at[c, k],
+            in_recv.at[c, k],
             device_id={"dp": partner},
             device_id_type=MESH,
         ).start()
-        F[rows, cols] = lax.dot_general(av[slot, :, :UNIT], gv[t % 2], dims, preferred_element_type=F32)
+        F[rows, cols] = lax.dot_general(av[slot, :, :UNIT], gv[mine], dims, preferred_element_type=F32)
 
     def hop_reduce(c, k, level, s, path):
         axis = ORDER[k][level]
@@ -237,11 +321,38 @@
             send(at(X, x_base, k, box), at(R, r_base, k, landing(k, level, way, step)), k, recv(level, step + 1), peer)
 
         def recv(lv, step):
-            first = {0: 1, 1: 1 + SIZE[ORDER[k][0]] // 2, 2: 1 + (SIZE[ORDER[k][0]] + SIZE[ORDER[k][1]]) // 2}[lv]
-            return hop_recv.at[c, k, first + step - 1]
+            return hop_recv.at[c, k, FIRST[lv] + step]
 
         def blk(o):
             return block(k, level, add(p, n, sg * o), within)
+
+        if level in DIRECT[k]:
+            if s == 0:
+                for o in range(1, n):
+                    box = block(k, level, add(p, n, o), within)
+                    put(box, None)
+                    send(
+                        at(X, x_base, k, box),
+                        at(R, r_base, k, landing_direct(k, level, o)),
+                        k,
+                        recv(level, 1),
+                        beside(axis, o),
+                    )
+            else:
+                box = blk(0)
+                arrived(box, n - 1, recv(level, 1))
+
+                def body(r):
+                    value = own(box, r)
+                    for o in range(1, n):
+                        value = value + got(landing_direct(k, level, o), r)
+                    if whole:
+                        at(G, g_base, k, box)[...] = value.astype(BF16)
+                    else:
+                        at(F, x_base, k, box)[...] = value
+
+                rows_loop(box.rows, body)
+            return
 
         if s > 0:
             one = blk(0)
@@ -292,11 +403,9 @@
         g_base = own_base(c)
         ups, downs, sg = (ahead, behind, sign) if whole else (up, down, 1)
         within = path[level - 1] if level else None
-        sizes = [SIZE[d] // 2 for d in ORDER[k]]
-        first = {2: 1 + sum(sizes), 1: 1 + sum(sizes) + sizes[2], 0: 1 + sum(sizes) + sizes[2] + sizes[1]}[level]
 
         def recv(step):
-            return hop_recv.at[c, k, first + step - 1]
+            return hop_recv.at[c, k, FIRST[level + 3] + step]
 
         def blk(o):
             return block(k, level, add(p, n, sg * o), within)
@@ -313,6 +422,14 @@
                     view, view, out_send, out_recv, device_id={"dp": partner}, device_id_type=MESH
                 ).start()
 
+        if level in DIRECT[k]:
+            if s == 0:
+                view = at(G, g_base, k, blk(0))
+                for o in range(1, n):
+                    send(view, view, k, recv(1), beside(axis, o))
+            else:
+                arrived(blk(0), n - 1, recv(1))
+            return
         if s == 0:
             go(blk(0), 0, 0)
             go(blk(0), 1, 0)
@@ -334,53 +451,47 @@
         across(from_below)
         across(from_above)
 
-    def plan(k):
-        sizes = [SIZE[d] // 2 for d in ORDER[k]]
-        steps = [[] for _ in range(HOPS)]
-        h = 0
+    def hop(c, k, h):
+        if h == 0:
+            view = X.at[pl.ds(0, UNIT), pl.ds(0, COLOUR)]
+            pltpu.make_async_copy(view, view, in_recv.at[c, k]).wait()
+            pltpu.make_async_copy(view, view, in_send.at[c, k]).wait()
+        path = []
         for level in range(3):
-            for s in range(sizes[level] + 1):
-                steps[h].append((hop_reduce, level, s))
-                h += s < sizes[level]
-        for level in (2, 1, 0):
-            for s in range(sizes[level] + 1):
-                steps[h].append((hop_gather, level, s))
-                h += s < sizes[level]
-        assert h == HOPS - 1
-        return steps
-
-    plans = [plan(k) for k in range(3)]
-
-    def hop(h, c):
-        if h == 0:
-            view = X.at[pl.ds(0, UNIT), :]
-            pltpu.make_async_copy(view, view, in_recv.at[c]).wait()
-            pltpu.make_async_copy(view, view, in_send.at[c]).wait()
-        for k in (2, 0, 1):
-            path = []
-            for level in range(3):
-                path.append(block(k, level, place[ORDER[k][level]], path[-1] if path else None))
-            for f, level, s in plans[k][h]:
-                f(c, k, level, s, path)
-
-    for copy in load_a(0, 0):
-        copy.start()
-    fetch(jnp.int32(0), 0)
-
-    where = [(pos(h) // 6, pos(h) % 6) for h in range(HOPS)]
-    last = max(j for j, _ in where)
-
-    def iteration(i, _):
-        for q in range(6):
-            pl.when(i < CHUNKS)(functools.partial(matmul, i, q))
-            for h in reversed(range(HOPS)):
-                j, at_q = where[h]
-                if at_q == q:
-                    c = i - j
-                    pl.when(jnp.logical_and(c >= 0, c < CHUNKS))(functools.partial(hop, h, c))
+            path.append(block(k, level, place[ORDER[k][level]], path[-1] if path else None))
+        for gather, level, s in plan(k, DIRECT[k])[h]:
+            (hop_gather if gather else hop_reduce)(c, k, level, s, path)
+
+    after = {}
+    tile = -1
+    for item in sequence():
+        if item is None:
+            tile += 1
+        else:
+            after.setdefault(tile, []).append(item)
+    tiles = CHUNKS * TILES
+    assert tile == tiles - 1 and min(after) > 0
+
+    def run(hops):
+        for c, k, h in hops:
+            hop(c, k, h)
+
+    def step(i, _):
+        matmul(i)
+        for c in range(CHUNKS):
+            mine = [j for j in after if j // TILES == c and j < tiles - 1]
+
+            def of_chunk(mine=mine):
+                for j in mine:
+                    pl.when(i == j)(functools.partial(run, after[j]))
+
+            if mine:
+                pl.when(i // TILES == c)(of_chunk)
         return 0
 
-    lax.fori_loop(0, CHUNKS + last, iteration, 0)
+    matmul(jnp.int32(0), first=True)
+    lax.fori_loop(1, tiles, step, 0)
+    run(after[tiles - 1])
 
     half = X.at[pl.ds(0, CHUNKS * UNIT), :]
     pltpu.make_async_copy(half, half, out_recv).wait()
@@ -406,15 +517,15 @@
             out_specs=pl.BlockSpec(memory_space=pltpu.VMEM),
             scratch_shapes=[
                 pltpu.VMEM((2, 2048, 2 * UNIT), BF16),
-                pltpu.VMEM((4, 2048, TILE), BF16),
+                pltpu.VMEM((LOADS, 2048, TILE), BF16),
                 pltpu.VMEM((CHUNKS * UNIT, WIDE), BF16),
                 pltpu.VMEM((CHUNKS * UNIT, WIDE), F32),
                 pltpu.VMEM((CHUNKS * SLOTS, WIDE), BF16),
                 dma((2, 2)),
-                dma((4,)),
-                dma((CHUNKS,)),
-                dma((CHUNKS,)),
-                dma((CHUNKS, 3, HOPS)),
+                dma((LOADS,)),
+                dma((CHUNKS, 3)),
+                dma((CHUNKS, 3)),
+                dma((CHUNKS, 3, 20)),
                 dma((3,)),
                 dma,
                 dma,

time: 152 us -> 129 us (0.85)
  Pallas kernels: 151 us -> 129 us
    pallas_call x1, Pallas kernels: 146 us -> 123 us  [body(): pl.pallas_call(kernel, out_shape=pltpu.VMEM((2 * CHUNKS * UNIT, WIDE), BF...]
where the time goes in v2:
time: 129 us
  Pallas kernels  129 us (100%)
    pallas_call x1, Pallas kernels, body(): pl.pallas_call(kernel, out_shape=pltpu.VMEM((2 * CHUNKS * UNIT, WIDE), BF...  123 us
    pallas_call x1, Pallas kernels, body(): pl.pallas_call(unload, out_shape=jax.ShapeDtypeStruct(held.shape, held.dt...  5.82 us

profile of v2, /device:TPU:1, one launch (start us, length us, event | category | flops | bytes accessed | tf_op | source)
XLA Modules:
  0.0 129.2 jit_solution(15548268446362090055)
XLA Ops:
  0.0 123.3 %sums.1.v = bf16[2560,3072]{1,0:T(8,128)(2,1)S(1)} custom-call(bf16[1,2,2048,1280]{3,2,1,0:T(8,128)(2,1)} %a.1, bf16[1,2,2048,3072]{3,2,1,0:T(8,128)(2,1)} %g.1), custom_call_target="tpu_custom_call" | custom-call | tf_op jit(solution)/shard_map/sums/pallas_call | solution.py:513
  123.4 5.8 %unload.1 = bf16[2560,3072]{1,0:T(8,128)(2,1)} custom-call(bf16[2560,3072]{1,0:T(8,128)(2,1)S(1)} %sums.1.v), custom_call_target="tpu_custom_call" | custom-call | tf_op jit(solution)/shard_map/unload/pallas_call | solution.py:538

commit v3 on v2

--- a/solution.py
+++ b/solution.py
@@ -21,6 +21,7 @@
 SLOTS = 272
 LOADS = 4
 AHEAD = 2
+PARTS = 8
 DIRECT = ((2,), (2,), (1, 2))
 
 
@@ -128,10 +129,10 @@
 
 
 def sequence():
-    latency, rate, tile_time, hop_time = 2.3, 46.6e3, 1.5, 0.035
+    latency, rate, tile_time, hop_time = 2.3, 46.6e3, 1.55, 0.035
     plans = [plan(k, DIRECT[k]) for k in range(3)]
     free, arrival, order = {}, {}, []
-    now, tile = 3.5, 0
+    now, tile = 4.7, 0
     while True:
         waiting = [x for x in arrival if arrival[x] is not None and x not in order]
         ready = [x for x in waiting if arrival[x] <= now]
@@ -152,7 +153,7 @@
             now += tile_time
             tile += 1
             if tile % (TILES // 3) == 0:
-                arrival[(tile - 1) // TILES, (tile - 1) % TILES // (TILES // 3), 0] = now + 1.8
+                arrival[(tile - 1) // TILES, ((tile - 1) % TILES // (TILES // 3) + 2) % 3, 0] = now + 1.8
         elif waiting:
             now = min(arrival[x] for x in waiting)
         else:
@@ -199,6 +200,9 @@
             )
         return copies
 
+    def columns(q):
+        return lax.rem(q + TILES // 3 * 2, TILES)
+
     def place_g(i, h):
         return lax.rem(i, AHEAD) + AHEAD * h
 
@@ -206,7 +210,7 @@
         c = i // TILES
         unit = 2 * c + (core if h == 0 else 1 - core)
         slot = place_g(i, h)
-        cols = pl.ds(pl.multiple_of(TILE * (i - TILES * c), TILE), TILE)
+        cols = pl.ds(pl.multiple_of(TILE * columns(i - TILES * c), TILE), TILE)
         return pltpu.make_async_copy(g.at[0, unit // 5, :, cols], gv.at[slot], g_sem.at[slot])
 
     def fetch(i):
@@ -269,6 +273,7 @@
         mine = place_g(i, 0)
         other = mine + jnp.where(c == 2, AHEAD, 0)
         rows = pl.ds(pl.multiple_of(UNIT * c, UNIT), UNIT)
+        q = columns(q)
         cols = pl.ds(pl.multiple_of(TILE * q, TILE), TILE)
         dims = (((0,), (0,)), ((), ()))
         theirs = lax.dot_general(av[slot, :, UNIT:], gv[other], dims, preferred_element_type=F32)
@@ -502,9 +507,14 @@
 
 
 def unload(v, o, sem):
-    copy = pltpu.make_async_copy(v, o, sem)
-    copy.start()
-    copy.wait()
+    rows = o.shape[0] // PARTS
+    copies = [
+        pltpu.make_async_copy(v.at[pl.ds(rows * i, rows)], o.at[pl.ds(rows * i, rows)], sem.at[i]) for i in range(PARTS)
+    ]
+    for copy in copies:
+        copy.start()
+    for copy in copies:
+        copy.wait()
 
 
 def solution(mesh):
@@ -540,7 +550,7 @@
             out_shape=jax.ShapeDtypeStruct(held.shape, held.dtype),
             in_specs=[pl.BlockSpec(memory_space=pltpu.VMEM)],
             out_specs=pl.BlockSpec(memory_space=pltpu.HBM),
-            scratch_shapes=[dma],
+            scratch_shapes=[dma((PARTS,))],
             compiler_params=pltpu.CompilerParams(vmem_limit_bytes=1 << 20),
             name="unload",
         )(held)

time: 129 us -> 127 us (0.984)
  Pallas kernels: 129 us -> 126 us
    pallas_call x1, Pallas kernels: 123 us -> 121 us  [body(): pl.pallas_call(kernel, out_shape=pltpu.VMEM((2 * CHUNKS * UNIT, WIDE), BF...]
where the time goes in v3:
time: 127 us; the launch traced here: 126 us
  Pallas kernels  126 us (99%)
    pallas_call x1, Pallas kernels, body(): pl.pallas_call(kernel, out_shape=pltpu.VMEM((2 * CHUNKS * UNIT, WIDE), BF...  121 us
    pallas_call x1, Pallas kernels, body(): pl.pallas_call(unload, out_shape=jax.ShapeDtypeStruct(held.shape, held.dt...  5.65 us

profile of v3, /device:TPU:1, one launch (start us, length us, event | category | flops | bytes accessed | tf_op | source)
XLA Modules:
  0.0 126.4 jit_solution(17527354400148022663)
XLA Ops:
  0.0 120.8 %sums.1.v = bf16[2560,3072]{1,0:T(8,128)(2,1)S(1)} custom-call(bf16[1,2,2048,1280]{3,2,1,0:T(8,128)(2,1)} %a.1, bf16[1,2,2048,3072]{3,2,1,0:T(8,128)(2,1)} %g.1), custom_call_target="tpu_custom_call" | custom-call | tf_op jit(solution)/shard_map/sums/pallas_call | solution.py:523
  120.8 5.6 %unload.1 = bf16[2560,3072]{1,0:T(8,128)(2,1)} custom-call(bf16[2560,3072]{1,0:T(8,128)(2,1)S(1)} %sums.1.v), custom_call_target="tpu_custom_call" | custom-call | tf_op jit(solution)/shard_map/unload/pallas_call | solution.py:548
